TPU v7x, 32 devices: a whole 2x2x4 slice. The times are simulated.
32 devices in a mesh: blk: 8 (over z, x), tgt: 4 (over y, core).
Axes of the slice: x: 2, y: 2, z: 4, core: 2. Of those that a mesh axis runs over, the one named last changes fastest.
Arguments:
- sources: float32 [8192, 128], P('blk'), may hold values from -0.5 to 0.5, as said below
- targets: float32 [8192, 128], P(('blk', 'tgt')), may hold values from -0.5 to 0.5, as said below
- duals_init: float32 [8192], P(('blk', 'tgt')), may hold values from -1.5 to 1.5
Outputs:
- source_duals: float32 [8192], P('blk')
- target_duals: float32 [8192], P(('blk', 'tgt'))
Inputs may be any that keep to these rules, and one draw needn't show every extreme that they name: `sources`: coordinates of the source points. `targets`: coordinates of the target points.
All inputs are finite; a program needn't handle non-finite values.
Results may differ from a plain program's by a relative error of at most 0.0001.
Values sent between devices are 32-bit elements; how exact they have to be, the bound alone decides.
A program may use at most 64 MiB of HBM per device.

v0:
```python
import jax
import jax.numpy as jnp
from jax import lax
from jax.sharding import PartitionSpec as P

ITERS = 2


EPS = 0.05


def cost_of(left, left_norm, right, right_norm):
    cross = jnp.dot(
        left, right.T, preferred_element_type=jnp.float32, precision=lax.Precision.HIGHEST
    )
    return left_norm[:, None] + right_norm[None, :] - 2.0 * cross


def body(sources, targets, duals_init):
    src_norm = jnp.sum(sources * sources, axis=1)
    rows_here = sources.shape[0]
    cols_here = targets.shape[0]
    total_dst = cols_here * lax.axis_size("blk") * lax.axis_size("tgt")
    total_src = rows_here * lax.axis_size("blk")
    target_pots = duals_init
    source_pots = jnp.zeros_like(src_norm)
    group_rows = lax.all_gather(targets, "blk", axis=0, tiled=True)
    group_norm = jnp.sum(group_rows * group_rows, axis=1)
    cost_tile = cost_of(sources, src_norm, group_rows, group_norm)
    for repeat in range(ITERS):
        group_pots = lax.all_gather(target_pots, "blk", axis=0, tiled=True)
        scores = (group_pots[None, :] - cost_tile) / EPS
        maxima = jnp.max(scores, axis=1)
        totals = jnp.sum(jnp.exp(scores - maxima[:, None]), axis=1)
        highest = lax.pmax(maxima, "tgt")
        totals = lax.psum(totals * jnp.exp(maxima - highest), "tgt")
        maxima = highest
        source_pots = EPS * -jnp.log(jnp.float32(total_dst)) - EPS * (maxima + jnp.log(totals))
        col_scores = (source_pots[:, None] - cost_tile) / EPS
        col_high = lax.pmax(jnp.max(col_scores, axis=0), "blk")
        col_part = jnp.sum(jnp.exp(col_scores - col_high[None, :]), axis=0)
        col_total = lax.psum_scatter(col_part, "blk", scatter_dimension=0, tiled=True)
        own_high = lax.dynamic_slice_in_dim(
            col_high, lax.axis_index("blk") * cols_here, cols_here, 0
        )
        target_pots = EPS * -jnp.log(jnp.float32(total_src)) - EPS * (own_high + jnp.log(col_total))
    return (source_pots, target_pots)


def solution(mesh):
    return jax.shard_map(
        body,
        mesh=mesh,
        in_specs=(P("blk", None), P(("blk", "tgt"), None), P(("blk", "tgt"))),
        out_specs=(P("blk"), P(("blk", "tgt"))),
        check_vma=False,
    )
```

profile of v0, /device:TPU:0, one launch (start us, length us, event | category | flops | bytes accessed | tf_op | source)
XLA Modules:
  0.0 220.8 jit_solution(6186228106651673261)
XLA Ops:
  7.2 0.0 all-gather.4.cloned.1.call-start
  7.2 0.7 all-gather.4.cloned.1.call-update
  7.9 1.2 dynamic-slice
  9.8 22.5 %all-gather = f32[8,1,256]{2,1,0:T(1,128)S(1)} all-gather(f32[1,1,256]{2,1,0:T(1,128)} %bitcast.12), channel_id=1, replica_groups=mesh['blk'=8,'tgt'=4] {'blk'}, dimensions={0}, use_global_device_ids=true | all-gather | bytes 9216 | tf_op jit(solution)/shard_map/all_gather | solution.py:31
  32.3 1.2 multiply_reduce_fusion.1
  33.6 19.5 %all-gather.4.cloned.1.call-done = f32[2048,128]{1,0:T(8,128)} async-done(((f32[256,128]{1,0:T(8,128)}), f32[2048,128]{1,0:T(8,128)}) %all-gather.4.cloned.1.call-update) | async-done | bytes 1048592 | tf_op jit(solution)/shard_map/all_gather | solution.py:27
  53.1 1.6 multiply_reduce_fusion
  54.7 11.5 %fusion = (f32[1024]{0:T(1024)S(1)}, f32[1024,2048]{1,0:T(8,128)}) fusion(f32[2048]{0:T(1024)S(1)} %bitcast.9, f32[1024,128]{1,0:T(8,128)} %param.3, f32[2048,128]{1,0:T(8,128)} %all-gather.4.cloned.1.call-done, f32[2048]{0:T(1024)S(1)} %multiply_reduce_fusion, f32[1024]{0:T(1024)S(1)} %multiply_reduce_fusion.1), kind=kOutput, calls=%fused_computation.9 | convolution fusion | flops 3233807360 | bytes 9986048 | tf_op jit(solution)/shard_map/dot_general | solution.py:13
  66.2 5.6 %pmax.28 = f32[1024]{0:T(1024)S(1)} all-reduce(f32[1024]{0:T(1024)S(1)} %get-tuple-element.2), channel_id=1, replica_groups=mesh['blk'=8,'tgt'=4] {'tgt'}, use_global_device_ids=true, to_apply=%region_3.0 | all-reduce | flops 1024 | bytes 8192 | tf_op jit(solution)/shard_map/pmax | solution.py:35
  71.8 4.5 %exponential_reduce_fusion.3 = f32[1024]{0:T(1024)S(1)} fusion(f32[1024,2048]{1,0:T(8,128)} %get-tuple-element.3, f32[1024]{0:T(1024)S(1)} %get-tuple-element.2, f32[2048]{0:T(1024)S(1)} %bitcast.10), kind=kLoop, calls=%fused_computation.6 | loop fusion | flops 8387584 | bytes 8404992 | tf_op jit(solution)/shard_map/reduce_sum | solution.py:34
  76.4 6.6 %psum.14 = f32[1024]{0:T(1024)S(1)} all-reduce(f32[1024]{0:T(1024)S(1)} %exponential_multiply_fusion.1), channel_id=1, replica_groups=mesh['blk'=8,'tgt'=4] {'tgt'}, use_global_device_ids=true, to_apply=%region_5.0 | all-reduce | flops 1024 | bytes 8192 | tf_op jit(solution)/shard_map/psum | solution.py:36
  83.0 4.3 %fusion.1 = f32[2048]{0:T(1024)S(1)} fusion(f32[1024,2048]{1,0:T(8,128)} %get-tuple-element.3, f32[1024]{0:T(1024)S(1)} %multiply_subtract_fusion.2), kind=kLoop, calls=%fused_computation.10 | loop fusion | flops 6289408 | bytes 8400896 | tf_op jit(solution)/shard_map/reduce_max | solution.py:40
  87.3 19.4 %pmax.29 = f32[2048]{0:T(1024)S(1)} all-reduce(f32[2048]{0:T(1024)S(1)} %fusion.1), channel_id=1, replica_groups=mesh['blk'=8,'tgt'=4] {'blk'}, use_global_device_ids=true, to_apply=%region_7.0 | all-reduce | flops 2048 | bytes 16384 | tf_op jit(solution)/shard_map/pmax | solution.py:40
  106.7 4.5 %exponential_reduce_fusion.2 = f32[2048]{0:T(1024)S(1)} fusion(f32[1024,2048]{1,0:T(8,128)} %get-tuple-element.3, f32[2048]{0:T(1024)S(1)} %pmax.29, f32[1024]{0:T(1024)S(1)} %multiply_subtract_fusion.2), kind=kLoop, calls=%fused_computation.4 | loop fusion | flops 8386560 | bytes 8409088 | tf_op jit(solution)/shard_map/reduce_sum | solution.py:41
  111.2 17.4 %all-reduce = f32[2048]{0:T(1024)S(1)} all-reduce(f32[2048]{0:T(1024)S(1)} %exponential_reduce_fusion.2), channel_id=2, replica_groups=mesh['blk'=8,'tgt'=4] {'blk'}, use_global_device_ids=true, to_apply=%region_9.0.clone | all-reduce | flops 2048 | bytes 16384
  128.6 0.1 fusion.9
  128.7 18.2 %all-gather.1 = f32[8,1,256]{2,1,0:T(1,128)S(1)} all-gather(f32[1,1,256]{2,1,0:T(1,128)S(1)} %bitcast.11), channel_id=1, replica_groups=mesh['blk'=8,'tgt'=4] {'blk'}, dimensions={0}, use_global_device_ids=true | all-gather | bytes 9216 | tf_op jit(solution)/shard_map/all_gather | solution.py:31
  147.0 4.3 %fusion.2 = f32[1024]{0:T(1024)S(1)} fusion(f32[1024,2048]{1,0:T(8,128)} %get-tuple-element.3, f32[2048]{0:T(1024)S(1)} %bitcast.7), kind=kLoop, calls=%fused_computation.11 | loop fusion | flops 6290432 | bytes 8400896 | tf_op jit(solution)/shard_map/reduce_max | solution.py:33
  151.3 4.5 %exponential_reduce_fusion.1 = f32[1024]{0:T(1024)S(1)} fusion(f32[1024,2048]{1,0:T(8,128)} %get-tuple-element.3, f32[1024]{0:T(1024)S(1)} %fusion.2, f32[2048]{0:T(1024)S(1)} %bitcast.8), kind=kLoop, calls=%fused_computation.2 | loop fusion | flops 8387584 | bytes 8404992 | tf_op jit(solution)/shard_map/reduce_sum | solution.py:34
  155.8 5.7 %pmax.30 = f32[1024]{0:T(1024)S(1)} all-reduce(f32[1024]{0:T(1024)S(1)} %fusion.2), channel_id=1, replica_groups=mesh['blk'=8,'tgt'=4] {'tgt'}, use_global_device_ids=true, to_apply=%region_11.0 | all-reduce | flops 1024 | bytes 8192 | tf_op jit(solution)/shard_map/pmax | solution.py:35
  161.5 6.3 %psum.15 = f32[1024]{0:T(1024)S(1)} all-reduce(f32[1024]{0:T(1024)S(1)} %exponential_multiply_fusion), channel_id=1, replica_groups=mesh['blk'=8,'tgt'=4] {'tgt'}, use_global_device_ids=true, to_apply=%region_13.0 | all-reduce | flops 1024 | bytes 8192 | tf_op jit(solution)/shard_map/psum | solution.py:36
  167.7 0.0 copy-start
  167.7 4.3 %fusion.3 = f32[2048]{0:T(1024)S(1)} fusion(f32[1024,2048]{1,0:T(8,128)} %get-tuple-element.3, f32[1024]{0:T(1024)S(1)} %multiply_subtract_fusion.1), kind=kLoop, calls=%fused_computation.12 | loop fusion | flops 6289408 | bytes 8400896 | tf_op jit(solution)/shard_map/reduce_max | solution.py:40
  172.0 17.4 %pmax.31 = f32[2048]{0:T(1024)S(1)} all-reduce(f32[2048]{0:T(1024)S(1)} %fusion.3), channel_id=1, replica_groups=mesh['blk'=8,'tgt'=4] {'blk'}, use_global_device_ids=true, to_apply=%region_15.0 | all-reduce | flops 2048 | bytes 16384 | tf_op jit(solution)/shard_map/pmax | solution.py:40
  189.4 4.5 %exponential_reduce_fusion = f32[2048]{0:T(1024)S(1)} fusion(f32[1024,2048]{1,0:T(8,128)} %get-tuple-element.3, f32[2048]{0:T(1024)S(1)} %pmax.31, f32[1024]{0:T(1024)S(1)} %multiply_subtract_fusion.1), kind=kLoop, calls=%fused_computation | loop fusion | flops 8386560 | bytes 8409088 | tf_op jit(solution)/shard_map/reduce_sum | solution.py:41
  193.9 0.0 copy-done
  193.9 19.4 %all-reduce.1 = f32[2048]{0:T(1024)S(1)} all-reduce(f32[2048]{0:T(1024)S(1)} %exponential_reduce_fusion), channel_id=3, replica_groups=mesh['blk'=8,'tgt'=4] {'blk'}, use_global_device_ids=true, to_apply=%region_17.0.clone | all-reduce | flops 2048 | bytes 16384
  213.3 0.7 fusion.6
  (4 shorter events, 0.0 us)
Async XLA Ops:
  7.2 46.0 %all-gather.4.cloned.1.call-start = ((), (), s32[]{:S(2)}) async-start(), calls=%async_computation | async-start | bytes 1179648 | tf_op jit(solution)/shard_map/all_gather | solution.py:27
  167.7 26.2 %copy-start = (f32[1024]{0:T(1024)}, f32[1024]{0:T(1024)S(1)}, u32[]{:S(2)}) copy-start(f32[1024]{0:T(1024)S(1)} %multiply_subtract_fusion.1) | copy-start | bytes 12292
Sparse Core Ops, SparseCore 0:
  10.1 42.9 all-gather.3
where the time goes:
time: 221 us
  blocking collectives  139 us (63%)
  other arithmetic  34.5 us (16%)
  waiting for transfers between devices  20.2 us (9%)
  between operations  14.8 us (7%)
  matrix products  11.5 us (5%)
    all_gather x2, blocking collectives, body(): group_pots = lax.all_gather(target_pots, 'blk', axis=0, tiled=True)  40.8 us
    unnamed x2, blocking collectives  36.8 us
    pmax x2, blocking collectives, body(): col_high = lax.pmax(jnp.max(col_scores, axis=0), 'blk')  36.8 us
    all_gather x1, waiting for transfers between devices, body(): group_rows = lax.all_gather(targets, 'blk', axis=0, tiled=True)  19.5 us
    psum x2, blocking collectives, body(): totals = lax.psum(totals * jnp.exp(maxima - highest), 'tgt')  12.9 us
    dot_general x1, matrix products, cost_of(): jnp.dot(left, right.T, preferred_element_type=jnp.float32, precision=lax....  11.5 us
    pmax x2, blocking collectives, body(): highest = lax.pmax(maxima, 'tgt')  11.3 us
    reduce_sum x2, other arithmetic, body(): totals = jnp.sum(jnp.exp(scores - maxima[:, None]), axis=1)  9.01 us
  transfers between devices with their start and end apart: 1, of which 1 were waited for; matrix products, arithmetic and copies ran while one was open for 1% of the time, Pallas kernels for 0%

commit v1 on v0

v1 whole, which is shorter than its diff:
```python
import functools
import math

import jax
import jax.numpy as jnp
from jax import lax
from jax.experimental import pallas as pl
from jax.experimental.pallas import tpu as pltpu
from jax.sharding import PartitionSpec as P

ITERS = 2
EPS = 0.05
LOG2E = math.log2(math.e)
SCALE = LOG2E / EPS
MESH = pl.DeviceIdType.MESH
LANES = 128
COLS_CHUNK_ROWS = 32
DOT_ROWS = 128


def log2_of(value):
    return jnp.log(value) * LOG2E


def pieces_of(value, count):
    parts = []
    for _ in range(count):
        part = value.astype(jnp.bfloat16)
        parts.append(part)
        value = value - part.astype(jnp.float32)
    return parts


def extended(points, scale, norm_first):
    norm = -SCALE * jnp.sum(points * points, axis=1, keepdims=True)
    hi, lo = pieces_of(points * scale, 2)
    first, second, third = (part.astype(jnp.float32) for part in pieces_of(norm, 3))
    lane = lax.broadcasted_iota(jnp.int32, points.shape, 1)
    base = 0 if norm_first else 3
    ones = 3 - base
    extra = jnp.where((lane >= ones) & (lane < ones + 3), 1.0, 0.0)
    extra = jnp.where(lane == base, first, extra)
    extra = jnp.where(lane == base + 1, second, extra)
    extra = jnp.where(lane == base + 2, third, extra)
    middle = (lo, hi) if norm_first else (hi, lo)
    return jnp.concatenate([hi, middle[0], middle[1], extra.astype(jnp.bfloat16)], axis=1)


def kernel(
    n_hi, n_th, src_ref, tgt_ref, dual_ref, src_out, tgt_out,
    src_in, left, right, cost, blocks, duals, top, acc, shift, pots, row_buf, col_buf, fin_mine, fin_buf, out_mine, out_buf,
    s_sem, z_send, z_recv, zd_send, zd_recv, f_send, f_recv, fd_send, fd_recv, r_send, r_recv, c_send, c_recv, o_sem,
):
    rows, width = src_ref.shape
    own = tgt_ref.shape[0]
    pair = 2 * own
    n_src = rows * n_hi * 2
    n_dst = own * n_hi * 2 * n_th * 2
    b, t = lax.axis_index("blk"), lax.axis_index("tgt")
    hi, lo = lax.div(b, 2), lax.rem(b, 2)
    th, tl = lax.div(t, 2), lax.rem(t, 2)

    def col_peer(dh, dl):
        return (lax.rem(hi + dh, n_hi) * 2 + lo, th * 2 + lax.rem(tl + dl, 2))

    def row_peer(dlo, dth):
        return (hi * 2 + lax.rem(lo + dlo, 2), lax.rem(th + dth, n_th) * 2 + tl)

    col_moves = [(dh, dl) for dh in range(n_hi) for dl in range(2) if dh or dl]
    row_moves = [(dlo, dth) for dlo in range(2) for dth in range(n_th) if dlo or dth]
    my_col = hi * 2 + tl
    my_row = lo * n_th + th

    def remote(src, dst, send, recv, peer):
        return pltpu.make_async_remote_copy(
            src_ref=src, dst_ref=dst, send_sem=send, recv_sem=recv, device_id=peer, device_id_type=MESH
        )

    barrier = pltpu.get_barrier_semaphore()
    peers = [col_peer(*move) for move in col_moves] + [row_peer(*move) for move in row_moves]
    for peer in peers:
        pl.semaphore_signal(barrier, inc=1, device_id=peer, device_id_type=MESH)

    def fill_left(ref):
        def step(index, carry):
            at = pl.ds(pl.multiple_of(index * LANES, LANES), LANES)
            left[at, :] = extended(ref[at, :], 1.0, True)
            return carry

        lax.fori_loop(0, rows // LANES, step, 0)

    pl.semaphore_wait(barrier, len(peers))

    has_rows = lo == tl
    swap = remote(src_ref, src_in, s_sem.at[0], s_sem.at[1], row_peer(1, 0))

    started = []
    z_copies, f_copies = {}, {}
    for dh in range(1, n_hi):
        z_copies[dh] = (
            remote(dual_ref, duals.at[hi, tl], zd_send.at[dh], zd_recv.at[dh], col_peer(dh, 0)),
            remote(tgt_ref, blocks.at[hi, tl], z_send.at[dh], z_recv.at[dh], col_peer(dh, 0)),
        )
        for copy in z_copies[dh]:
            copy.start()

    @pl.when(has_rows)
    def _():
        swap.start()

    f_copies[0] = (
        remote(dual_ref, duals.at[hi, tl], fd_send.at[0], fd_recv.at[0], col_peer(0, 1)),
        remote(tgt_ref, blocks.at[hi, tl], f_send.at[0], f_recv.at[0], col_peer(0, 1)),
    )
    for copy in f_copies[0]:
        copy.start()
    blocks[hi, tl] = tgt_ref[...]
    duals[hi, tl] = dual_ref[...]

    @pl.when(has_rows)
    def _():
        fill_left(src_ref)

    @pl.when(jnp.logical_not(has_rows))
    def _():
        swap.wait_recv()
        fill_left(src_in)

    def use_pair(h, first):
        for c in range(2):
            right[c * own : (c + 1) * own, :] = extended(blocks[h, c], 2.0 * SCALE, False)
        pots_here = SCALE * jnp.concatenate([duals[h, 0], duals[h, 1]], axis=1)

        def step(index, carry):
            at = pl.ds(pl.multiple_of(index * DOT_ROWS, DOT_ROWS), DOT_ROWS)
            tile = lax.dot_general(
                left[at, :], right[...], (((1,), (1,)), ((), ())), preferred_element_type=jnp.float32
            )
            cost[h, at, :] = tile
            scores = [
                tile[:, k : k + LANES] + pots_here[:, k : k + LANES] for k in range(0, pair, LANES)
            ]
            high = functools.reduce(jnp.maximum, scores)
            if not first:
                before = top[at, :]
                high = jnp.maximum(high, before)
            total = sum(jnp.exp2(score - high) for score in scores)
            if not first:
                total = total + acc[at, :] * jnp.exp2(before - high)
            top[at, :] = high
            acc[at, :] = total
            return carry

        lax.fori_loop(0, rows // DOT_ROWS, step, 0)

    for dh in range(n_hi):
        h = lax.rem(hi + n_hi - dh, n_hi)
        if dh:
            for copy in z_copies[dh]:
                copy.wait_recv()
            f_copies[dh] = (
                remote(duals.at[h, tl], duals.at[h, tl], fd_send.at[dh], fd_recv.at[dh], col_peer(0, 1)),
                remote(blocks.at[h, tl], blocks.at[h, tl], f_send.at[dh], f_recv.at[dh], col_peer(0, 1)),
            )
            for copy in f_copies[dh]:
                copy.start()
        for copy in f_copies[dh]:
            copy.wait_recv()
        use_pair(h, dh == 0)

    def row_pass():
        def step(index, carry):
            at = pl.ds(pl.multiple_of(index * 8, 8), 8)
            scores = [
                cost[h, at, k : k + LANES] + pots[h : h + 1, k : k + LANES]
                for h in range(n_hi)
                for k in range(0, pair, LANES)
            ]
            high = functools.reduce(jnp.maximum, scores)
            top[at, :] = high
            acc[at, :] = sum(jnp.exp2(score - high) for score in scores)
            return carry

        lax.fori_loop(0, rows // 8, step, 0, unroll=2)

    def col_pass(h):
        groups = COLS_CHUNK_ROWS // 8

        def step(index, carry):
            high, total = carry
            at = pl.ds(pl.multiple_of(index * COLS_CHUNK_ROWS, COLS_CHUNK_ROWS), COLS_CHUNK_ROWS)
            offs = shift[at, :]
            new_high, new_total = [], []
            tile = cost[h, at, :]
            for k in range(pair // LANES):
                scores = tile[:, k * LANES : (k + 1) * LANES] + offs
                parts = [scores[g * 8 : (g + 1) * 8] for g in range(groups)]
                best = jnp.maximum(high[k], functools.reduce(jnp.maximum, parts))
                part = sum(jnp.exp2(value - best) for value in parts)
                new_total.append(total[k] * jnp.exp2(high[k] - best) + part)
                new_high.append(best)
            return tuple(new_high), tuple(new_total)

        lowest = tuple(jnp.full((8, LANES), -1e38, jnp.float32) for _ in range(pair // LANES))
        zero = tuple(jnp.zeros((8, LANES), jnp.float32) for _ in range(pair // LANES))
        high, total = lax.fori_loop(0, rows // COLS_CHUNK_ROWS, step, (lowest, zero), unroll=2)
        high, total = jnp.concatenate(high, axis=1), jnp.concatenate(total, axis=1)
        best = jnp.max(high, axis=0, keepdims=True)
        return best + log2_of(jnp.sum(total * jnp.exp2(high - best), axis=0, keepdims=True))

    def joined(values):
        best = functools.reduce(jnp.maximum, values)
        return best + log2_of(sum(jnp.exp2(value - best) for value in values))

    pending = []
    for turn in range(ITERS):
        last = turn == ITERS - 1
        if turn:
            row_pass()
        for k in range(rows // LANES):
            high = top[k * LANES : (k + 1) * LANES, :].T
            total = acc[k * LANES : (k + 1) * LANES, :].T
            best = jnp.max(high, axis=0, keepdims=True)
            total = jnp.sum(total * jnp.exp2(high - best), axis=0, keepdims=True)
            row_buf[turn, my_row, k : k + 1, :] = best + log2_of(total)
        copies = []
        for index, move in enumerate(row_moves):
            mine = row_buf.at[turn, my_row]
            copies.append(remote(mine, mine, r_send.at[turn, index], r_recv.at[turn, index], row_peer(*move)))
            copies[-1].start()
        for copy in copies:
            copy.wait_recv()
        pending += copies
        offs = -math.log2(n_dst) - joined([row_buf[turn, g] for g in range(2 * n_th)])
        if last:
            out_mine[...] = offs * (1.0 / SCALE)
            hand = remote(out_mine, out_buf, o_sem.at[0], o_sem.at[1], col_peer(0, 1))

            @pl.when(has_rows)
            def _():
                hand.start()

        for k in range(rows // LANES):
            spread = jnp.broadcast_to(offs[k : k + 1, :], (LANES, LANES))
            shift[k * LANES : (k + 1) * LANES, :] = spread.T
        if not last:
            for h in range(n_hi):
                col_buf[turn, my_col, h : h + 1, :] = col_pass(h)
            copies = []
            for index, move in enumerate(col_moves):
                mine = col_buf.at[turn, my_col]
                copies.append(remote(mine, mine, c_send.at[turn, index], c_recv.at[turn, index], col_peer(*move)))
                copies[-1].start()
            for copy in copies:
                copy.wait_recv()
            pending += copies
            pots[...] = -math.log2(n_src) - joined([col_buf[turn, g] for g in range(2 * n_hi)])
        else:
            for h in range(n_hi):
                value = col_pass(h)
                for c in range(2):
                    fin_mine[h, c] = value[:, c * own : (c + 1) * own]
            copies = []
            for index, (dh, dl) in enumerate(col_moves):
                mine = fin_mine.at[lax.rem(hi + dh, n_hi), lax.rem(tl + dl, 2)]
                copies.append(
                    remote(mine, fin_buf.at[my_col], c_send.at[turn, index], c_recv.at[turn, index], col_peer(dh, dl))
                )
                copies[-1].start()
            fin_buf[my_col] = fin_mine[hi, tl]
            for copy in copies:
                copy.wait_recv()
            pending += copies
            value = -math.log2(n_src) - joined([fin_buf[g] for g in range(2 * n_hi)])
            tgt_out[...] = value * (1.0 / SCALE)

    @pl.when(has_rows)
    def _():
        src_out[...] = out_mine[...]
        hand.wait_send()
        swap.wait_send()

    @pl.when(jnp.logical_not(has_rows))
    def _():
        hand.wait_recv()
        src_out[...] = out_buf[...]

    for group in list(z_copies.values()) + list(f_copies.values()):
        for copy in group:
            copy.wait_send()
    for copy in pending:
        copy.wait_send()


def body(sources, targets, duals_init, n_hi, n_th):
    rows, width = sources.shape
    own = targets.shape[0]
    pair = 2 * own
    vmem = pl.BlockSpec(memory_space=pltpu.VMEM)
    dma = pltpu.SemaphoreType.DMA
    f32 = jnp.float32
    source_pots, target_pots = pl.pallas_call(
        functools.partial(kernel, n_hi, n_th),
        out_shape=(
            jax.ShapeDtypeStruct((rows // LANES, LANES), f32),
            jax.ShapeDtypeStruct((1, own), f32),
        ),
        in_specs=[vmem] * 3,
        out_specs=(vmem, vmem),
        scratch_shapes=[
            pltpu.VMEM((rows, width), f32),
            pltpu.VMEM((rows, 4 * width), jnp.bfloat16),
            pltpu.VMEM((pair, 4 * width), jnp.bfloat16),
            pltpu.VMEM((n_hi, rows, pair), f32),
            pltpu.VMEM((n_hi, 2, own, width), f32),
            pltpu.VMEM((n_hi, 2, 1, own), f32),
            pltpu.VMEM((rows, LANES), f32),
            pltpu.VMEM((rows, LANES), f32),
            pltpu.VMEM((rows, LANES), f32),
            pltpu.VMEM((n_hi, pair), f32),
            pltpu.VMEM((ITERS, 2 * n_th, rows // LANES, LANES), f32),
            pltpu.VMEM((ITERS, 2 * n_hi, n_hi, pair), f32),
            pltpu.VMEM((n_hi, 2, 1, own), f32),
            pltpu.VMEM((2 * n_hi, 1, own), f32),
            pltpu.VMEM((rows // LANES, LANES), f32),
            pltpu.VMEM((rows // LANES, LANES), f32),
            dma((2,)),
            dma((n_hi,)), dma((n_hi,)), dma((n_hi,)), dma((n_hi,)),
            dma((n_hi,)), dma((n_hi,)), dma((n_hi,)), dma((n_hi,)),
            dma((ITERS, 2 * n_th)), dma((ITERS, 2 * n_th)),
            dma((ITERS, 2 * n_hi)), dma((ITERS, 2 * n_hi)),
            dma((2,)),
        ],
        compiler_params=pltpu.CompilerParams(
            collective_id=0, has_side_effects=True, vmem_limit_bytes=60 * 1024 * 1024
        ),
    )(sources, targets, duals_init.reshape(1, own))
    return source_pots.reshape(rows), target_pots.reshape(own)


def solution(mesh):
    n_hi, n_th = mesh.shape["blk"] // 2, mesh.shape["tgt"] // 2
    return jax.shard_map(
        functools.partial(body, n_hi=n_hi, n_th=n_th),
        mesh=mesh,
        in_specs=(P("blk", None), P(("blk", "tgt"), None), P(("blk", "tgt"))),
        out_specs=(P("blk"), P(("blk", "tgt"))),
        check_vma=False,
    )
```

time: 221 us -> 57 us (0.26)
  blocking collectives: 139 us -> 0 us
  Pallas kernels: 0 us -> 54.3 us
  other arithmetic: 34.5 us -> 0 us
  waiting for transfers between devices: 20.2 us -> 0 us
  between operations: 14.8 us -> 0.65 us
  matrix products: 11.5 us -> 0 us
    pallas_call x0 -> x1, Pallas kernels: none -> 54.3 us  [body(): pl.pallas_call(functools.partial(kernel, n_hi, n_th), out_shape=(jax.Shap...]
    pmax x4 -> x0, blocking collectives: 48.1 us -> none  [the longest x2 36.8 us: body(): col_high = lax.pmax(jnp.max(col_scores, axis=0), 'blk')]
    all_gather x2 -> x0, blocking collectives: 40.8 us -> none  [body(): group_pots = lax.all_gather(target_pots, 'blk', axis=0, tiled=True)]
    unnamed x2 -> x0, blocking collectives: 36.8 us -> none
    reduce_sum x6 -> x0, other arithmetic: 20.8 us -> none  [the longest x2 9.01 us: body(): totals = jnp.sum(jnp.exp(scores - maxima[:, None]), axis=1)]
    all_gather x1 -> x0, waiting for transfers between devices: 19.5 us -> none  [body(): group_rows = lax.all_gather(targets, 'blk', axis=0, tiled=True)]
    psum x2 -> x0, blocking collectives: 12.9 us -> none  [body(): totals = lax.psum(totals * jnp.exp(maxima - highest), 'tgt')]
    reduce_max x3 -> x0, other arithmetic: 12.9 us -> none  [the longest x2 8.56 us: body(): col_high = lax.pmax(jnp.max(col_scores, axis=0), 'blk')]
  transfers between devices with their start and end apart: 1 -> 0, of which waited for: 1 -> 0; matrix products, arithmetic and copies ran while one was open for 1% -> 0% of each run, Pallas kernels for 0% -> 0%
where the time goes in v1:
time: 57 us; the launch traced here: 56.8 us
  Pallas kernels  54.3 us (95%)
  local copies, waits for them, and re-layouts  1.87 us (3%)
  between operations  0.65 us (1%)
    pallas_call x1, Pallas kernels, body(): pl.pallas_call(functools.partial(kernel, n_hi, n_th), out_shape=(jax.Shap...  54.3 us
    unnamed x6, local copies, waits for them, and re-layouts  1.87 us

profile of v1, /device:TPU:0, one launch (start us, length us, event | category | flops | bytes accessed | tf_op | source)
XLA Modules:
  0.0 56.8 jit_solution(11023960149086459385)
XLA Ops:
  0.6 54.3 %shard_map.50 = (f32[8,128]{1,0:T(8,128)}, f32[1,256]{1,0:T(1,128)}) custom-call(f32[1024,128]{1,0:T(8,128)} %src_ref.1, f32[256,128]{1,0:T(8,128)} %tgt_ref.1, f32[1,256]{1,0:T(1,128)} %bitcast.4), custom_call_target="tpu_custom_call" | custom-call | tf_op jit(solution)/shard_map/pallas_call | solution.py:302
  55.0 0.0 copy-start
  55.0 0.7 %copy-done = f32[8,128]{1,0:T(8,128)S(1)} copy-done((f32[8,128]{1,0:T(8,128)S(1)}, f32[8,128]{1,0:T(8,128)}, u32[]{:S(2)}) %copy-start) | copy-done | bytes 4120
  55.6 0.0 copy-start.1
  55.6 0.6 %copy.7 = f32[1024]{0:T(1024)} copy(f32[1024]{0:T(1024)S(1)} %bitcast.3) | data formatting | bytes 8192
  56.2 0.0 copy-done.1
  56.3 0.6 copy.8
Async XLA Ops:
  55.0 0.7 %copy-start = (f32[8,128]{1,0:T(8,128)S(1)}, f32[8,128]{1,0:T(8,128)}, u32[]{:S(2)}) copy-start(f32[8,128]{1,0:T(8,128)} %get-tuple-element.4) | copy-start | bytes 12292
  55.6 0.6 %copy-start.1 = (f32[1,256]{1,0:T(1,128)S(1)}, f32[1,256]{1,0:T(1,128)}, u32[]{:S(2)}) copy-start(f32[1,256]{1,0:T(1,128)} %get-tuple-element.5) | copy-start | bytes 3076

commit v2 on v1

--- a/solution.py
+++ b/solution.py
@@ -15,7 +15,8 @@
 MESH = pl.DeviceIdType.MESH
 LANES = 128
 COLS_CHUNK_ROWS = 32
-DOT_ROWS = 128
+DOT_ROWS = 512
+SWAPS = 4
 
 
 def log2_of(value):
@@ -49,7 +50,7 @@
 def kernel(
     n_hi, n_th, src_ref, tgt_ref, dual_ref, src_out, tgt_out,
     src_in, left, right, cost, blocks, duals, top, acc, shift, pots, row_buf, col_buf, fin_mine, fin_buf, out_mine, out_buf,
-    s_sem, z_send, z_recv, zd_send, zd_recv, f_send, f_recv, fd_send, fd_recv, r_send, r_recv, c_send, c_recv, o_sem,
+    s_send, s_recv, z_send, z_recv, zd_send, zd_recv, f_send, f_recv, fd_send, fd_recv, r_send, r_recv, c_send, c_recv, o_sem,
 ):
     rows, width = src_ref.shape
     own = tgt_ref.shape[0]
@@ -81,64 +82,89 @@
     for peer in peers:
         pl.semaphore_signal(barrier, inc=1, device_id=peer, device_id_type=MESH)
 
-    def fill_left(ref):
+    ordered = [jnp.int32(0)] * (n_hi - 1)
+    found = jnp.int32(0)
+    for distance in range(1, n_hi):
+        for place in (hi - distance, hi + distance):
+            valid = jnp.where((place >= 0) & (place < n_hi), 1, 0)
+            for k in range(n_hi - 1):
+                ordered[k] = ordered[k] + jnp.where(found == k, 1, 0) * valid * place
+            found = found + valid
+
+    def z_peer(place):
+        return (place * 2 + lo, t)
+
+    piece = rows // SWAPS
+
+    def fill_left(ref, part):
         def step(index, carry):
-            at = pl.ds(pl.multiple_of(index * LANES, LANES), LANES)
+            at = pl.ds(pl.multiple_of(part * piece + index * LANES, LANES), LANES)
             left[at, :] = extended(ref[at, :], 1.0, True)
             return carry
 
-        lax.fori_loop(0, rows // LANES, step, 0)
+        lax.fori_loop(0, piece // LANES, step, 0)
 
     pl.semaphore_wait(barrier, len(peers))
 
     has_rows = lo == tl
-    swap = remote(src_ref, src_in, s_sem.at[0], s_sem.at[1], row_peer(1, 0))
-
-    started = []
-    z_copies, f_copies = {}, {}
-    for dh in range(1, n_hi):
-        z_copies[dh] = (
-            remote(dual_ref, duals.at[hi, tl], zd_send.at[dh], zd_recv.at[dh], col_peer(dh, 0)),
-            remote(tgt_ref, blocks.at[hi, tl], z_send.at[dh], z_recv.at[dh], col_peer(dh, 0)),
-        )
-        for copy in z_copies[dh]:
+    other = 1 - tl
+    swaps = []
+    for part in range(SWAPS):
+        at = pl.ds(part * piece, piece)
+        swaps.append(remote(src_ref.at[at], src_in.at[at], s_send.at[part], s_recv.at[part], row_peer(1, 0)))
+
+    def moves_to(block, dual, place, core, send, recv, d_send, d_recv, peer):
+        return (
+            remote(dual, duals.at[place, core], d_send, d_recv, peer),
+            remote(block, blocks.at[place, core], send, recv, peer),
+        )
+
+    def f_move(place, own_block):
+        block = tgt_ref if own_block else blocks.at[place, tl]
+        dual = dual_ref if own_block else duals.at[place, tl]
+        return moves_to(
+            block, dual, place, tl, f_send.at[place], f_recv.at[place], fd_send.at[place], fd_recv.at[place], col_peer(0, 1)
+        )
+
+    def f_arrival(place):
+        return moves_to(
+            tgt_ref, dual_ref, place, other, f_send.at[place], f_recv.at[place], fd_send.at[place], fd_recv.at[place], col_peer(0, 1)
+        )
+
+    sent = [
+        moves_to(
+            tgt_ref, dual_ref, hi, tl, z_send.at[k], z_recv.at[hi], zd_send.at[k], zd_recv.at[hi], z_peer(ordered[k])
+        )
+        for k in range(n_hi - 1)
+    ]
+    sent.append(f_move(hi, True))
+    for group in sent[-1:] + sent[:-1]:
+        for copy in group:
             copy.start()
 
     @pl.when(has_rows)
     def _():
-        swap.start()
-
-    f_copies[0] = (
-        remote(dual_ref, duals.at[hi, tl], fd_send.at[0], fd_recv.at[0], col_peer(0, 1)),
-        remote(tgt_ref, blocks.at[hi, tl], f_send.at[0], f_recv.at[0], col_peer(0, 1)),
-    )
-    for copy in f_copies[0]:
-        copy.start()
+        for copy in swaps:
+            copy.start()
+
     blocks[hi, tl] = tgt_ref[...]
     duals[hi, tl] = dual_ref[...]
 
-    @pl.when(has_rows)
-    def _():
-        fill_left(src_ref)
-
-    @pl.when(jnp.logical_not(has_rows))
-    def _():
-        swap.wait_recv()
-        fill_left(src_in)
-
-    def use_pair(h, first):
-        for c in range(2):
-            right[c * own : (c + 1) * own, :] = extended(blocks[h, c], 2.0 * SCALE, False)
-        pots_here = SCALE * jnp.concatenate([duals[h, 0], duals[h, 1]], axis=1)
+    def set_right(h, c):
+        right[...] = extended(blocks[h, c], 2.0 * SCALE, False)
+
+    def use_block(h, c, first, start, count):
+        pots_here = SCALE * duals[h, c]
+        chunk = min(DOT_ROWS, count)
 
         def step(index, carry):
-            at = pl.ds(pl.multiple_of(index * DOT_ROWS, DOT_ROWS), DOT_ROWS)
+            at = pl.ds(pl.multiple_of(start + index * chunk, chunk), chunk)
             tile = lax.dot_general(
                 left[at, :], right[...], (((1,), (1,)), ((), ())), preferred_element_type=jnp.float32
             )
-            cost[h, at, :] = tile
+            cost[h, c, at, :] = tile
             scores = [
-                tile[:, k : k + LANES] + pots_here[:, k : k + LANES] for k in range(0, pair, LANES)
+                tile[:, k : k + LANES] + pots_here[:, k : k + LANES] for k in range(0, own, LANES)
             ]
             high = functools.reduce(jnp.maximum, scores)
             if not first:
@@ -151,30 +177,50 @@
             acc[at, :] = total
             return carry
 
-        lax.fori_loop(0, rows // DOT_ROWS, step, 0)
-
-    for dh in range(n_hi):
-        h = lax.rem(hi + n_hi - dh, n_hi)
-        if dh:
-            for copy in z_copies[dh]:
-                copy.wait_recv()
-            f_copies[dh] = (
-                remote(duals.at[h, tl], duals.at[h, tl], fd_send.at[dh], fd_recv.at[dh], col_peer(0, 1)),
-                remote(blocks.at[h, tl], blocks.at[h, tl], f_send.at[dh], f_recv.at[dh], col_peer(0, 1)),
-            )
-            for copy in f_copies[dh]:
-                copy.start()
-        for copy in f_copies[dh]:
+        lax.fori_loop(0, count // chunk, step, 0)
+
+    set_right(hi, tl)
+    for part in range(SWAPS):
+
+        @pl.when(has_rows)
+        def _(part=part):
+            fill_left(src_ref, part)
+
+        @pl.when(jnp.logical_not(has_rows))
+        def _(part=part):
+            swaps[part].wait_recv()
+            fill_left(src_in, part)
+
+        use_block(hi, tl, True, part * piece, piece)
+    for copy in f_arrival(hi):
+        copy.wait_recv()
+    set_right(hi, other)
+    use_block(hi, other, False, 0, rows)
+
+    for k in range(n_hi - 1):
+        place = ordered[k]
+        for copy in moves_to(
+            tgt_ref, dual_ref, place, tl, z_send.at[k], z_recv.at[place], zd_send.at[k], zd_recv.at[place], z_peer(place)
+        ):
             copy.wait_recv()
-        use_pair(h, dh == 0)
+        sent.append(f_move(place, False))
+        for copy in sent[-1]:
+            copy.start()
+        set_right(place, tl)
+        use_block(place, tl, False, 0, rows)
+        for copy in f_arrival(place):
+            copy.wait_recv()
+        set_right(place, other)
+        use_block(place, other, False, 0, rows)
 
     def row_pass():
         def step(index, carry):
             at = pl.ds(pl.multiple_of(index * 8, 8), 8)
             scores = [
-                cost[h, at, k : k + LANES] + pots[h : h + 1, k : k + LANES]
+                cost[h, c, at, k : k + LANES] + pots[h : h + 1, c * own + k : c * own + k + LANES]
                 for h in range(n_hi)
-                for k in range(0, pair, LANES)
+                for c in range(2)
+                for k in range(0, own, LANES)
             ]
             high = functools.reduce(jnp.maximum, scores)
             top[at, :] = high
@@ -191,7 +237,7 @@
             at = pl.ds(pl.multiple_of(index * COLS_CHUNK_ROWS, COLS_CHUNK_ROWS), COLS_CHUNK_ROWS)
             offs = shift[at, :]
             new_high, new_total = [], []
-            tile = cost[h, at, :]
+            tile = jnp.concatenate([cost[h, 0, at, :], cost[h, 1, at, :]], axis=1)
             for k in range(pair // LANES):
                 scores = tile[:, k * LANES : (k + 1) * LANES] + offs
                 parts = [scores[g * 8 : (g + 1) * 8] for g in range(groups)]
@@ -233,7 +279,7 @@
         pending += copies
         offs = -math.log2(n_dst) - joined([row_buf[turn, g] for g in range(2 * n_th)])
         if last:
-            out_mine[...] = offs * (1.0 / SCALE)
+            out_mine[...] = offs
             hand = remote(out_mine, out_buf, o_sem.at[0], o_sem.at[1], col_peer(0, 1))
 
             @pl.when(has_rows)
@@ -272,20 +318,21 @@
                 copy.wait_recv()
             pending += copies
             value = -math.log2(n_src) - joined([fin_buf[g] for g in range(2 * n_hi)])
-            tgt_out[...] = value * (1.0 / SCALE)
+            tgt_out[...] = value
 
     @pl.when(has_rows)
     def _():
         src_out[...] = out_mine[...]
         hand.wait_send()
-        swap.wait_send()
+        for copy in swaps:
+            copy.wait_send()
 
     @pl.when(jnp.logical_not(has_rows))
     def _():
         hand.wait_recv()
         src_out[...] = out_buf[...]
 
-    for group in list(z_copies.values()) + list(f_copies.values()):
+    for group in sent:
         for copy in group:
             copy.wait_send()
     for copy in pending:
@@ -310,8 +357,8 @@
         scratch_shapes=[
             pltpu.VMEM((rows, width), f32),
             pltpu.VMEM((rows, 4 * width), jnp.bfloat16),
-            pltpu.VMEM((pair, 4 * width), jnp.bfloat16),
-            pltpu.VMEM((n_hi, rows, pair), f32),
+            pltpu.VMEM((own, 4 * width), jnp.bfloat16),
+            pltpu.VMEM((n_hi, 2, rows, own), f32),
             pltpu.VMEM((n_hi, 2, own, width), f32),
             pltpu.VMEM((n_hi, 2, 1, own), f32),
             pltpu.VMEM((rows, LANES), f32),
@@ -324,7 +371,7 @@
             pltpu.VMEM((2 * n_hi, 1, own), f32),
             pltpu.VMEM((rows // LANES, LANES), f32),
             pltpu.VMEM((rows // LANES, LANES), f32),
-            dma((2,)),
+            dma((SWAPS,)), dma((SWAPS,)),
             dma((n_hi,)), dma((n_hi,)), dma((n_hi,)), dma((n_hi,)),
             dma((n_hi,)), dma((n_hi,)), dma((n_hi,)), dma((n_hi,)),
             dma((ITERS, 2 * n_th)), dma((ITERS, 2 * n_th)),
@@ -335,7 +382,7 @@
             collective_id=0, has_side_effects=True, vmem_limit_bytes=60 * 1024 * 1024
         ),
     )(sources, targets, duals_init.reshape(1, own))
-    return source_pots.reshape(rows), target_pots.reshape(own)
+    return source_pots.reshape(rows) * (1.0 / SCALE), target_pots.reshape(own) * (1.0 / SCALE)
 
 
 def solution(mesh):

time: 57 us -> 50.6 us (0.89)
  Pallas kernels: 54.3 us -> 47.9 us
  local copies, waits for them, and re-layouts: 1.87 us -> 0.01 us
  other arithmetic: 0 us -> 1.83 us
    pallas_call x1, Pallas kernels: 54.3 us -> 47.9 us  [body(): pl.pallas_call(functools.partial(kernel, n_hi, n_th), out_shape=(jax.Shap...]
    unnamed x6 -> x2, local copies, waits for them, and re-layouts: 1.87 us -> 0.01 us
    mul x0 -> x2, other arithmetic: none -> 1.83 us  [the longest x1 1.27 us: body(): source_pots.reshape(rows) * (1.0 / SCALE)]
where the time goes in v2:
time: 50.6 us; the launch traced here: 50.4 us
  Pallas kernels  47.9 us (95%)
  other arithmetic  1.83 us (4%)
  between operations  0.65 us (1%)
    pallas_call x1, Pallas kernels, body(): pl.pallas_call(functools.partial(kernel, n_hi, n_th), out_shape=(jax.Shap...  47.9 us
    mul x1, other arithmetic, body(): source_pots.reshape(rows) * (1.0 / SCALE)  1.27 us

profile of v2, /device:TPU:0, one launch (start us, length us, event | category | flops | bytes accessed | tf_op | source)
XLA Modules:
  0.0 50.4 jit_solution(10723219909487851269)
XLA Ops:
  0.6 47.9 %shard_map.50 = (f32[8,128]{1,0:T(8,128)}, f32[1,256]{1,0:T(1,128)}) custom-call(f32[1024,128]{1,0:T(8,128)} %src_ref.1, f32[256,128]{1,0:T(8,128)} %tgt_ref.1, f32[1,256]{1,0:T(1,128)} %bitcast.4), custom_call_target="tpu_custom_call" | custom-call | tf_op jit(solution)/shard_map/pallas_call | solution.py:349
  48.6 0.0 copy-start
  48.6 1.3 %multiply_bitcast_fusion = f32[1024]{0:T(1024)} fusion(f32[8,128]{1,0:T(8,128)} %get-tuple-element.4), kind=kLoop, calls=%fused_computation | loop fusion | flops 1024 | bytes 8192 | tf_op jit(solution)/shard_map/mul | solution.py:385
  49.9 0.0 copy-done
  49.9 0.6 %broadcast_multiply_fusion = f32[1,256]{1,0:T(1,128)} fusion(f32[1,256]{1,0:T(1,128)S(1)} %copy-done), kind=kLoop, calls=%fused_computation.1 | loop fusion | flops 256 | bytes 2048 | tf_op jit(solution)/shard_map/mul | solution.py:385
Async XLA Ops:
  48.6 1.3 %copy-start = (f32[1,256]{1,0:T(1,128)S(1)}, f32[1,256]{1,0:T(1,128)}, u32[]{:S(2)}) copy-start(f32[1,256]{1,0:T(1,128)} %get-tuple-element.5) | copy-start | bytes 3076

commit v3 on v2

--- a/solution.py
+++ b/solution.py
@@ -14,7 +14,7 @@
 SCALE = LOG2E / EPS
 MESH = pl.DeviceIdType.MESH
 LANES = 128
-COLS_CHUNK_ROWS = 32
+COLS_CHUNK_ROWS = 128
 DOT_ROWS = 512
 SWAPS = 4
 
@@ -104,9 +104,21 @@
 
         lax.fori_loop(0, piece // LANES, step, 0)
 
+    def set_right(h, c):
+        right[...] = extended(blocks[h, c], 2.0 * SCALE, False)
+
+    has_rows = lo == tl
+    blocks[hi, tl] = tgt_ref[...]
+    duals[hi, tl] = dual_ref[...]
+    set_right(hi, tl)
+
+    @pl.when(has_rows)
+    def _():
+        for part in range(SWAPS):
+            fill_left(src_ref, part)
+
     pl.semaphore_wait(barrier, len(peers))
 
-    has_rows = lo == tl
     other = 1 - tl
     swaps = []
     for part in range(SWAPS):
@@ -146,12 +158,6 @@
     def _():
         for copy in swaps:
             copy.start()
-
-    blocks[hi, tl] = tgt_ref[...]
-    duals[hi, tl] = dual_ref[...]
-
-    def set_right(h, c):
-        right[...] = extended(blocks[h, c], 2.0 * SCALE, False)
 
     def use_block(h, c, first, start, count):
         pots_here = SCALE * duals[h, c]
@@ -179,12 +185,7 @@
 
         lax.fori_loop(0, count // chunk, step, 0)
 
-    set_right(hi, tl)
     for part in range(SWAPS):
-
-        @pl.when(has_rows)
-        def _(part=part):
-            fill_left(src_ref, part)
 
         @pl.when(jnp.logical_not(has_rows))
         def _(part=part):
@@ -227,7 +228,7 @@
             acc[at, :] = sum(jnp.exp2(score - high) for score in scores)
             return carry
 
-        lax.fori_loop(0, rows // 8, step, 0, unroll=2)
+        lax.fori_loop(0, rows // 8, step, 0, unroll=16)
 
     def col_pass(h):
         groups = COLS_CHUNK_ROWS // 8
@@ -249,7 +250,7 @@
 
         lowest = tuple(jnp.full((8, LANES), -1e38, jnp.float32) for _ in range(pair // LANES))
         zero = tuple(jnp.zeros((8, LANES), jnp.float32) for _ in range(pair // LANES))
-        high, total = lax.fori_loop(0, rows // COLS_CHUNK_ROWS, step, (lowest, zero), unroll=2)
+        high, total = lax.fori_loop(0, rows // COLS_CHUNK_ROWS, step, (lowest, zero), unroll=4)
         high, total = jnp.concatenate(high, axis=1), jnp.concatenate(total, axis=1)
         best = jnp.max(high, axis=0, keepdims=True)
         return best + log2_of(jnp.sum(total * jnp.exp2(high - best), axis=0, keepdims=True))

time: 50.6 us -> 47.3 us (0.935)
  Pallas kernels: 47.9 us -> 44.6 us
    pallas_call x1, Pallas kernels: 47.9 us -> 44.6 us  [body(): pl.pallas_call(functools.partial(kernel, n_hi, n_th), out_shape=(jax.Shap...]
where the time goes in v3:
time: 47.3 us; the launch traced here: 47.1 us
  Pallas kernels  44.6 us (94%)
  other arithmetic  1.83 us (4%)
  between operations  0.65 us (1%)
    pallas_call x1, Pallas kernels, body(): pl.pallas_call(functools.partial(kernel, n_hi, n_th), out_shape=(jax.Shap...  44.6 us
    mul x1, other arithmetic, body(): source_pots.reshape(rows) * (1.0 / SCALE)  1.27 us

profile of v3, /device:TPU:0, one launch (start us, length us, event | category | flops | bytes accessed | tf_op | source)
XLA Modules:
  0.0 47.1 jit_solution(13438390663822869832)
XLA Ops:
  0.6 44.6 %shard_map.50 = (f32[8,128]{1,0:T(8,128)}, f32[1,256]{1,0:T(1,128)}) custom-call(f32[1024,128]{1,0:T(8,128)} %src_ref.1, f32[256,128]{1,0:T(8,128)} %tgt_ref.1, f32[1,256]{1,0:T(1,128)} %bitcast.4), custom_call_target="tpu_custom_call" | custom-call | tf_op jit(solution)/shard_map/pallas_call | solution.py:350
  45.3 0.0 copy-start
  45.3 1.3 %multiply_bitcast_fusion = f32[1024]{0:T(1024)} fusion(f32[8,128]{1,0:T(8,128)} %get-tuple-element.4), kind=kLoop, calls=%fused_computation | loop fusion | flops 1024 | bytes 8192 | tf_op jit(solution)/shard_map/mul | solution.py:386
  46.5 0.0 copy-done
  46.5 0.6 %broadcast_multiply_fusion = f32[1,256]{1,0:T(1,128)} fusion(f32[1,256]{1,0:T(1,128)S(1)} %copy-done), kind=kLoop, calls=%fused_computation.1 | loop fusion | flops 256 | bytes 2048 | tf_op jit(solution)/shard_map/mul | solution.py:386
Async XLA Ops:
  45.3 1.3 %copy-start = (f32[1,256]{1,0:T(1,128)S(1)}, f32[1,256]{1,0:T(1,128)}, u32[]{:S(2)}) copy-start(f32[1,256]{1,0:T(1,128)} %get-tuple-element.5) | copy-start | bytes 3076
